TPU v7x, 256 devices: a whole 4x4x8 slice. The times are simulated.
256 devices in a mesh: lon: 64 (over x, z, core), lat: 4 (over y).
Axes of the slice: x: 4, y: 4, z: 8, core: 2. Of those that a mesh axis runs over, the one named last changes fastest.
Arguments:
- state: float32 [2048, 64, 1024], P('lon', None, 'lat'), may hold values from -6 to 6
Outputs:
- spectrum: float32 [2, 1024, 64, 1024], P(None, 'lon', None, 'lat')
All inputs are finite; a program needn't handle non-finite values.
Results may differ from a plain program's by a relative error of at most 0.00011.
Values sent between devices are 32-bit elements; how exact they have to be, the bound alone decides.
A program may use at most 64 MiB of HBM per device.

v0:
```python
import math

import jax
import jax.numpy as jnp
from jax import lax
from jax.sharding import PartitionSpec as P


def phase_angle(first_index, second_index, period):
    product = first_index * second_index % period
    return product.astype(jnp.float32) * (2.0 * math.pi / period)


def factored_spectrum(gathered, factor):
    lon_count, width = gathered.shape
    bit_total = lon_count.bit_length() - 1
    outer = 2 ** (bit_total // 2)
    inner = lon_count // outer
    kept = inner // 2
    blocks = gathered.reshape(outer, inner, width)
    angle_first = phase_angle(
        lax.broadcasted_iota(jnp.int32, (outer, outer), 0),
        lax.broadcasted_iota(jnp.int32, (outer, outer), 1),
        outer,
    )
    first_re = jnp.einsum(
        "an,nbr->abr", jnp.cos(angle_first), blocks, precision=lax.Precision.HIGHEST
    )
    first_im = jnp.einsum(
        "an,nbr->abr", -jnp.sin(angle_first), blocks, precision=lax.Precision.HIGHEST
    )
    angle_turn = phase_angle(
        lax.broadcasted_iota(jnp.int32, (outer, inner), 0),
        lax.broadcasted_iota(jnp.int32, (outer, inner), 1),
        lon_count,
    )[:, :, None]
    cos_turn = jnp.cos(angle_turn)
    sin_turn = jnp.sin(angle_turn)
    turned_re = first_re * cos_turn + first_im * sin_turn
    turned_im = first_im * cos_turn - first_re * sin_turn
    angle_second = phase_angle(
        lax.broadcasted_iota(jnp.int32, (kept, inner), 0),
        lax.broadcasted_iota(jnp.int32, (kept, inner), 1),
        inner,
    )
    cos_second = jnp.cos(angle_second) * factor
    sin_second = jnp.sin(angle_second) * factor
    out_re = jnp.einsum(
        "cb,abr->car", cos_second, turned_re, precision=lax.Precision.HIGHEST
    ) + jnp.einsum("cb,abr->car", sin_second, turned_im, precision=lax.Precision.HIGHEST)
    out_im = jnp.einsum(
        "cb,abr->car", cos_second, turned_im, precision=lax.Precision.HIGHEST
    ) - jnp.einsum("cb,abr->car", sin_second, turned_re, precision=lax.Precision.HIGHEST)
    return jnp.stack([out_re, out_im]).reshape(2, kept * outer, width)


def local(state):
    lon_dev, fields, lat_dev = state.shape
    devices = lax.axis_size("lon")
    columns = state.reshape(lon_dev, fields * lat_dev)
    factor = 1.0 / math.sqrt(lon_dev * devices)
    gathered = lax.all_to_all(columns, "lon", split_axis=1, concat_axis=0, tiled=True)
    spectrum = factored_spectrum(gathered, factor)
    shares = lax.all_to_all(spectrum, "lon", split_axis=1, concat_axis=2, tiled=True)
    return shares.reshape(2, shares.shape[1], fields, lat_dev)


def solution(mesh):
    return jax.shard_map(
        local,
        mesh=mesh,
        in_specs=(P("lon", None, "lat"),),
        out_specs=P(None, "lon", None, "lat"),
        check_vma=False,
    )
```

profile of v0, /device:TPU:1, one launch (start us, length us, event | category | flops | bytes accessed | tf_op | source)
XLA Modules:
  0.0 147.2 jit_solution(2070723789590345443)
XLA Ops:
  0.0 4.1 %copy.20 = f32[32,64,256]{2,0,1:T(8,128)} copy(f32[32,64,256]{2,1,0:T(8,128)} %param.1) | data formatting | bytes 4194304 | tf_op args[0]
  4.1 13.2 %all-to-all-start = ((f32[32,64,256]{2,0,1:T(8,128)}), f32[32,64,256]{2,0,1:T(8,128)S(1)}, u32[]{:S(2)}, u32[]{:S(2)}) async-start(f32[32,64,256]{2,0,1:T(8,128)} %copy.20), calls=%async_computation | async-start | bytes 4194304 | tf_op jit(solution)/shard_map/all_to_all | solution.py:62
  17.3 0.1 fusion.55
  17.4 0.1 copy.22
  17.5 0.1 fusion.54
  17.5 0.1 copy.24
  17.6 50.7 %all-to-all-done = f32[32,64,256]{2,0,1:T(8,128)S(1)} async-done(((f32[32,64,256]{2,0,1:T(8,128)}), f32[32,64,256]{2,0,1:T(8,128)S(1)}, u32[]{:S(2)}, u32[]{:S(2)}) %all-to-all-start) | async-done | bytes 2097184 | tf_op jit(solution)/shard_map/all_to_all | solution.py:62
  68.3 3.0 %fusion.10 = f32[32,64,256]{2,0,1:T(8,128)S(1)} fusion(f32[32,64,256]{2,1,0:T(8,128)S(1)} %bitcast.26), kind=kOutput, calls=%fused_computation.13 | convolution fusion | flops 201340928 | bytes 4194304 | tf_op jit(solution)/shard_map/an,nbr->abr/dot_general | solution.py:26
  71.3 3.6 %multiply_add_fusion = (f32[32,64,256]{2,0,1:T(8,128)S(1)}, f32[32,64,256]{2,0,1:T(8,128)S(1)}) fusion(f32[32,64,256]{2,0,1:T(8,128)S(1)} %fusion.10, f32[32,64]{0,1:T(8,128)S(1)} %copy.24, f32[32,64]{0,1:T(8,128)S(1)} %copy.22, f32[32,64,256]{2,1,0:T(8,128)S(1)} %bitcast.27), kind=kOutput, calls=%fused_computation.2 | convolution fusion | flops 204487680 | bytes 8404992 | tf_op jit(solution)/shard_map/an,nbr->abr/dot_general | solution.py:29
  74.9 2.4 %fusion = f32[32,32,256]{2,0,1:T(8,128)S(1)} fusion(f32[32,64,256]{2,0,1:T(8,128)S(1)} %get-tuple-element.6), kind=kOutput, calls=%fused_computation.3 | convolution fusion | flops 201357312 | bytes 3145728 | tf_op jit(solution)/shard_map/cb,abr->car/dot_general | solution.py:51
  77.3 2.4 %fusion.2 = f32[32,32,256]{2,0,1:T(8,128)S(1)} fusion(f32[32,64,256]{2,0,1:T(8,128)S(1)} %get-tuple-element.6), kind=kOutput, calls=%fused_computation.5 | convolution fusion | flops 201357312 | bytes 3145728 | tf_op jit(solution)/shard_map/cb,abr->car/dot_general | solution.py:50
  79.7 2.6 %fusion.12 = f32[32,32,256]{2,0,1:T(8,128)S(1)} fusion(f32[32,32,256]{2,0,1:T(8,128)S(1)} %fusion.2, f32[32,64,256]{2,0,1:T(8,128)S(1)} %get-tuple-element.5), kind=kOutput, calls=%fused_computation.15 | convolution fusion | flops 201619456 | bytes 4194304 | tf_op jit(solution)/shard_map/cb,abr->car/dot_general | solution.py:48
  82.2 2.4 %fusion.15 = f32[32,32,256]{2,0,1:T(8,128)S(1)} fusion(f32[32,32,256]{2,0,1:T(8,128)S(1)} %fusion, f32[32,64,256]{2,0,1:T(8,128)S(1)} %get-tuple-element.5), kind=kOutput, calls=%fused_computation.16 | convolution fusion | flops 201619456 | bytes 4194304 | tf_op jit(solution)/shard_map/cb,abr->car/dot_general | solution.py:53
  84.6 0.6 copy.30
  85.2 0.6 copy.27
  85.8 0.1 pad_maximum_fusion
  86.0 1.6 %copy.31 = f32[2,1024,256]{2,0,1:T(2,128)S(1)} copy(f32[2,1024,256]{2,1,0:T(8,128)S(1)} %pad_maximum_fusion) | data formatting | bytes 4194304 | tf_op jit(solution)/shard_map/stack | solution.py:54
  87.6 56.8 %all_to_all.28 = f32[2,1024,256]{2,0,1:T(2,128)S(1)} all-to-all(f32[2,1024,256]{2,0,1:T(2,128)S(1)} %copy.31), channel_id=1, replica_groups=mesh['lon'=64,'lat'=4] {'lon'}, dimensions={1} | all-to-all | bytes 4194304 | tf_op jit(solution)/shard_map/all_to_all | solution.py:64
  144.4 0.2 copy.32
  144.6 2.5 %copy.33 = f32[2,16,64,256]{3,2,1,0:T(8,128)} copy(f32[2,16,64,256]{3,1,2,0:T(8,128)S(1)} %bitcast.28) | data formatting | bytes 4194304 | tf_op jit(solution)/shard_map/all_to_all | solution.py:64
Async XLA Ops:
  4.1 64.2 %all-to-all-start = ((f32[32,64,256]{2,0,1:T(8,128)}), f32[32,64,256]{2,0,1:T(8,128)S(1)}, u32[]{:S(2)}, u32[]{:S(2)}) async-start(f32[32,64,256]{2,0,1:T(8,128)} %copy.20), calls=%async_computation | async-start | bytes 4194304 | tf_op jit(solution)/shard_map/all_to_all | solution.py:62
where the time goes:
time: 147 us
  blocking collectives  56.8 us (39%)
  waiting for transfers between devices  50.7 us (34%)
  matrix products  16.2 us (11%)
  starting transfers between devices  13.2 us (9%)
  local copies, waits for them, and re-layouts  9.82 us (7%)
    all_to_all x1, blocking collectives, local(): lax.all_to_all(spectrum, 'lon', split_axis=1, concat_axis=2, tiled=True)  56.8 us
    all_to_all x1, waiting for transfers between devices, local(): lax.all_to_all(columns, 'lon', split_axis=1, concat_axis=0, tiled=True)  50.7 us
    all_to_all x1, starting transfers between devices, local(): lax.all_to_all(columns, 'lon', split_axis=1, concat_axis=0, tiled=True)  13.2 us
    unnamed x1, local copies, waits for them, and re-layouts  4.13 us
    dot_general x1, matrix products, factored_spectrum(): jnp.einsum('an,nbr->abr', -jnp.sin(angle_first), blocks, precision=lax.Pr...  3.57 us
    dot_general x1, matrix products, factored_spectrum(): jnp.einsum('an,nbr->abr', jnp.cos(angle_first), blocks, precision=lax.Pre...  3.02 us
  transfers between devices with their start and end apart: 1, of which 1 were waited for; matrix products, arithmetic and copies ran while one was open for 0% of the time, Pallas kernels for 0%

commit v1 on v0

v1 whole, which is shorter than its diff:
```python
import functools
import math

import jax
import jax.numpy as jnp
import numpy as np
from jax import lax
from jax.experimental import pallas as pl
from jax.experimental.pallas import tpu as pltpu
from jax.sharding import PartitionSpec as P

MESH = pl.DeviceIdType.MESH


def split_rows(matrix):
    high = matrix.astype(np.float32).astype(jnp.bfloat16)
    low = (matrix - high.astype(np.float64)).astype(np.float32).astype(jnp.bfloat16)
    return np.concatenate([high, low, high], axis=-1)


def tables(devices, depth):
    count, half, kept = devices * depth, devices // 2, depth // 2
    pair = np.arange(half, dtype=np.int64)
    d = np.arange(devices, dtype=np.int64)
    angle = 2.0 * math.pi / devices * (pair[:, None] * d[None, :] % devices)
    even, odd = np.cos(angle), -np.sin(angle)
    odd[0] = np.where(d % 2 == 0, 1.0, -1.0)
    first = np.concatenate([even, odd])
    j = np.arange(depth, dtype=np.int64)
    high = np.arange(kept, dtype=np.int64)
    second = np.zeros((half, 4 * kept, 2 * depth))
    scale = 1.0 / math.sqrt(count)

    def waves(low):
        turn = 2.0 * math.pi / count * ((low + devices * high)[:, None] * j[None, :] % count)
        return np.cos(turn) * scale, np.sin(turn) * scale

    for p in range(half):
        cos, sin = waves(p)
        if p == 0:
            cos_other, sin_other = waves(half)
            zero = np.zeros_like(cos)
            blocks = [[cos, zero], [-sin, zero], [zero, cos_other], [zero, -sin_other]]
        else:
            cos_other, sin_other = waves(devices - p)
            blocks = [[cos, sin], [-sin, cos], [cos_other, -sin_other], [-sin_other, -cos_other]]
        second[p] = np.block(blocks)
    return split_rows(first), split_rows(second)


def split_data(values):
    high = values.astype(jnp.bfloat16)
    low = (values - high.astype(jnp.float32)).astype(jnp.bfloat16)
    return jnp.concatenate([high, high, low], axis=0)


def kernel(
    sizes, x_hbm, first_hbm, second_hbm, out_hbm, x, g, middle, o, first, second, load_sem, send_sem, recv_sem
):
    xs, zs, cores, chunks = sizes
    devices = xs * zs * cores
    others = devices - 1
    depth, fields, lats = x_hbm.shape
    width = lats // chunks
    kept = depth // 2
    half = devices // 2

    me = lax.axis_index("lon")
    my_x, my_z, my_core = me // (zs * cores), me // cores % zs, me % cores

    def zigzag(step, size):
        odd = step % 2
        return size // 2 + (1 - odd) * (step // 2) - odd * ((step + 1) // 2)

    def peer(i):
        outer, dz = i // zs, zigzag(i % zs, zs)
        dx, dc = zigzag(outer // cores, xs), cores - 1 - outer % cores
        return (my_x + dx) % xs * (zs * cores) + (my_z + dz) % zs * cores + (my_core + dc) % cores

    load = pltpu.make_async_copy(x_hbm, x, load_sem.at[0])
    load.start()
    for chunk in range(chunks):
        lanes = pl.ds(chunk * width, width)
        pltpu.make_async_copy(x_hbm.at[:, me, lanes], g.at[:, me, lanes], recv_sem.at[0, chunk]).start()
    load_first = pltpu.make_async_copy(first_hbm, first, load_sem.at[1])
    load_first.start()
    load_second = pltpu.make_async_copy(second_hbm, second, load_sem.at[2])
    load_second.start()

    barrier = pltpu.get_barrier_semaphore()

    def greet(i, carry):
        pl.semaphore_signal(barrier, inc=1, device_id={"lon": peer(i)}, device_id_type=MESH)
        return carry

    lax.fori_loop(0, others, greet, 0)
    pl.semaphore_wait(barrier, others)
    load.wait()

    for chunk in range(chunks):
        lanes = pl.ds(chunk * width, width)

        def send_in(i, carry):
            to = peer(i)
            pltpu.make_async_remote_copy(
                src_ref=x.at[:, to, lanes],
                dst_ref=g.at[:, me, lanes],
                send_sem=send_sem.at[0],
                recv_sem=recv_sem.at[0, chunk],
                device_id={"lon": to},
                device_id_type=MESH,
            ).start()
            return carry

        lax.fori_loop(0, others, send_in, 0)

    load_first.wait()
    load_second.wait()

    for chunk in range(chunks):
        lanes = pl.ds(chunk * width, width)
        arrived = g.at[:, :, lanes]
        pltpu.make_async_copy(arrived, arrived, recv_sem.at[0, chunk]).wait()

        def stage_one(step, carry):
            matrix = first[...]
            for inner in range(2):
                j = step * 4 + inner * 2
                both = jnp.concatenate([g[j, :, lanes], g[j + 1, :, lanes]], axis=1)
                result = jnp.dot(matrix, split_data(both), preferred_element_type=jnp.float32)
                middle[pl.ds(pl.multiple_of(j * devices, devices), devices), :] = result[:, :width]
                middle[pl.ds(pl.multiple_of((j + 1) * devices, devices), devices), :] = result[:, width:]
            return carry

        lax.fori_loop(0, depth // 4, stage_one, 0)

        def stage_two(step, carry):
            for inner in range(4):
                p = step * 4 + inner
                other = (devices - p) % devices + half * ((half - 1 - p) // (half - 1))
                even = middle[pl.ds(p, depth, stride=devices), :]
                odd = middle[pl.ds(p + half, depth, stride=devices), :]
                data = split_data(jnp.concatenate([even, odd], axis=0))
                result = jnp.dot(second[p], data, preferred_element_type=jnp.float32)
                o[0, p, :, lanes] = result[:kept]
                o[1, p, :, lanes] = result[kept : 2 * kept]
                o[0, other, :, lanes] = result[2 * kept : 3 * kept]
                o[1, other, :, lanes] = result[3 * kept :]
            return carry

        lax.fori_loop(0, half // 4, stage_two, 0)

        blocks = devices // kept

        def send_out(i, carry):
            to = peer(i)
            pltpu.make_async_remote_copy(
                src_ref=o.at[:, pl.ds(to % blocks * kept, kept), to // blocks, lanes],
                dst_ref=out_hbm.at[:, :, me, lanes],
                send_sem=send_sem.at[1],
                recv_sem=recv_sem.at[1, chunk],
                device_id={"lon": to},
                device_id_type=MESH,
            ).start()
            return carry

        lax.fori_loop(0, others, send_out, 0)
        pltpu.make_async_copy(
            o.at[:, pl.ds(me % blocks * kept, kept), me // blocks, lanes],
            out_hbm.at[:, :, me, lanes],
            recv_sem.at[1, chunk],
        ).start()

    for chunk in range(chunks):
        lanes = pl.ds(chunk * width, width)
        landed = out_hbm.at[:, :, :, lanes]
        pltpu.make_async_copy(landed, landed, recv_sem.at[1, chunk]).wait()
    sent = o.at[:, pl.ds(0, others)]
    pltpu.make_async_copy(sent, sent, send_sem.at[0]).wait()
    pltpu.make_async_copy(sent, sent, send_sem.at[1]).wait()


def solution(mesh):
    devices = mesh.shape["lon"]
    sizes = (4, devices // 8, 2, 2)

    def local(state):
        depth, fields, lats = state.shape
        chunks = sizes[3]
        kept = depth // 2
        first, second = tables(devices, depth)
        return pl.pallas_call(
            functools.partial(kernel, sizes),
            out_shape=jax.ShapeDtypeStruct((2, kept, fields, lats), jnp.float32),
            in_specs=[pl.BlockSpec(memory_space=pl.ANY)] * 3,
            out_specs=pl.BlockSpec(memory_space=pl.ANY),
            scratch_shapes=[
                pltpu.VMEM((depth, fields, lats), jnp.float32),
                pltpu.VMEM((depth, devices, lats), jnp.float32),
                pltpu.VMEM((depth * devices, lats // chunks), jnp.float32),
                pltpu.VMEM((2, devices, kept, lats), jnp.float32),
                pltpu.VMEM(first.shape, jnp.bfloat16),
                pltpu.VMEM(second.shape, jnp.bfloat16),
                pltpu.SemaphoreType.DMA((3,)),
                pltpu.SemaphoreType.DMA((2,)),
                pltpu.SemaphoreType.DMA((2, chunks)),
            ],
            compiler_params=pltpu.CompilerParams(
                collective_id=0, has_side_effects=True, vmem_limit_bytes=56 * 1024 * 1024
            ),
            name="spectrum",
        )(state, jnp.asarray(first), jnp.asarray(second))

    return jax.shard_map(
        local,
        mesh=mesh,
        in_specs=(P("lon", None, "lat"),),
        out_specs=P(None, "lon", None, "lat"),
        check_vma=False,
    )
```

time: 147 us -> 105 us (0.71)
  Pallas kernels: 0 us -> 102 us
  blocking collectives: 56.8 us -> 0 us
  waiting for transfers between devices: 50.7 us -> 0 us
  matrix products: 16.2 us -> 0 us
  starting transfers between devices: 13.2 us -> 0 us
  local copies, waits for them, and re-layouts: 9.82 us -> 3.13 us
    pallas_call x0 -> x1, Pallas kernels: none -> 102 us  [local(): pl.pallas_call(functools.partial(kernel, sizes), out_shape=jax.ShapeDtype...]
    all_to_all x1 -> x0, blocking collectives: 56.8 us -> none  [local(): lax.all_to_all(spectrum, 'lon', split_axis=1, concat_axis=2, tiled=True)]
    all_to_all x1 -> x0, waiting for transfers between devices: 50.7 us -> none  [local(): lax.all_to_all(columns, 'lon', split_axis=1, concat_axis=0, tiled=True)]
    dot_general x6 -> x0, matrix products: 16.2 us -> none  [the longest x1 3.57 us: factored_spectrum(): jnp.einsum('an,nbr->abr', -jnp.sin(angle_first), blocks, precision=lax.Pr...]
    all_to_all x1 -> x0, starting transfers between devices: 13.2 us -> none  [local(): lax.all_to_all(columns, 'lon', split_axis=1, concat_axis=0, tiled=True)]
    all_to_all x2 -> x0, local copies, waits for them, and re-layouts: 2.7 us -> none  [local(): lax.all_to_all(spectrum, 'lon', split_axis=1, concat_axis=2, tiled=True)]
    another operation x1 -> x0, local copies, waits for them, and re-layouts: 1.62 us -> none  [factored_spectrum(): return jnp.stack([out_re, out_im]).reshape(2, kept * outer, width)]
  transfers between devices with their start and end apart: 1 -> 0, of which waited for: 1 -> 0; matrix products, arithmetic and copies ran while one was open for 0% -> 0% of each run, Pallas kernels for 0% -> 0%
where the time goes in v1:
time: 105 us
  Pallas kernels  102 us (97%)
  local copies, waits for them, and re-layouts  3.13 us (3%)
    pallas_call x1, Pallas kernels, local(): pl.pallas_call(functools.partial(kernel, sizes), out_shape=jax.ShapeDtype...  102 us
    unnamed x1, local copies, waits for them, and re-layouts  3.13 us

profile of v1, /device:TPU:1, one launch (start us, length us, event | category | flops | bytes accessed | tf_op | source)
XLA Modules:
  0.0 105.2 jit_solution(9985261070437169844)
XLA Ops:
  0.0 102.1 %spectrum.1 = f32[2,16,64,256]{3,2,1,0:T(8,128)} custom-call(f32[32,64,256]{2,1,0:T(8,128)} %x_hbm.1, bf16[64,192]{1,0:T(8,128)(2,1)} %constant.4.clone.first_hbm, bf16[32,64,192]{2,1,0:T(8,128)(2,1)} %constant.5.clone.second_hbm), custom_call_target="tpu_custom_call" | custom-call | tf_op jit(solution)/shard_map/spectrum/pallas_call | solution.py:192
  102.1 3.1 %copy.5 = f32[2,16,64,256]{3,2,1,0:T(8,128)} copy(f32[2,16,64,256]{3,2,1,0:T(8,128)} %spectrum.1) | data formatting | bytes 4194304

commit v2 on v1

--- a/solution.py
+++ b/solution.py
@@ -54,10 +54,44 @@
     return jnp.concatenate([high, high, low], axis=0)
 
 
-def kernel(
-    sizes, x_hbm, first_hbm, second_hbm, out_hbm, x, g, middle, o, first, second, load_sem, send_sem, recv_sem
-):
-    xs, zs, cores, chunks = sizes
+SEND_FROM_HBM = False
+BOTH = 1
+IN_ORDERS = ("near", "near")
+OUT_ORDERS = ("mixback", "mixback")
+
+
+def ring(step, size):
+    return min(step % size, -step % size)
+
+
+def arrange(shape, order):
+    xs, zs, cores = shape
+    offsets = [
+        (dx, dz, dc)
+        for dc in range(cores)
+        for dx in sorted(range(xs), key=lambda d: (ring(d, xs), d))
+        for dz in sorted(range(zs), key=lambda d: (ring(d, zs), d))
+    ][1:]
+    distance = lambda o: ring(o[0], xs) + ring(o[1], zs) + o[2]
+    if order == "near":
+        return sorted(offsets, key=distance)
+    if order == "far":
+        return sorted(offsets, key=distance, reverse=True)
+    if order == "zfar":
+        return sorted(offsets, key=lambda o: ring(o[1], zs), reverse=True)
+    if order == "znear":
+        return sorted(offsets, key=lambda o: ring(o[1], zs))
+    return offsets[::-1] if order == "mixback" else offsets
+
+
+def steps_away(offset, shape):
+    hops = ring(offset[0], shape[0]) + ring(offset[1], shape[1])
+    return max(hops, 1)
+
+
+def kernel(sizes, x_hbm, first_hbm, second_hbm, out, x, g, middle, o, first, second, load_sem, send_sem, recv_sem, ready_sem):
+    *shape, chunks = sizes
+    xs, zs, cores = shape
     devices = xs * zs * cores
     others = devices - 1
     depth, fields, lats = x_hbm.shape
@@ -67,52 +101,72 @@
 
     me = lax.axis_index("lon")
     my_x, my_z, my_core = me // (zs * cores), me // cores % zs, me % cores
-
-    def zigzag(step, size):
-        odd = step % 2
-        return size // 2 + (1 - odd) * (step // 2) - odd * ((step + 1) // 2)
-
-    def peer(i):
-        outer, dz = i // zs, zigzag(i % zs, zs)
-        dx, dc = zigzag(outer // cores, xs), cores - 1 - outer % cores
-        return (my_x + dx) % xs * (zs * cores) + (my_z + dz) % zs * cores + (my_core + dc) % cores
-
-    load = pltpu.make_async_copy(x_hbm, x, load_sem.at[0])
-    load.start()
+    part_x = [(my_x + d) % xs * (zs * cores) for d in range(xs)]
+    part_z = [(my_z + d) % zs * cores for d in range(zs)]
+    part_core = [(my_core + d) % cores for d in range(cores)]
+
+    def peer(offset):
+        dx, dz, dc = offset
+        return part_x[dx] + part_z[dz] + part_core[dc]
+
+    neighbours = [n for n in arrange(shape, "near") if steps_away(n, shape) == 1]
+
+    barrier = pltpu.get_barrier_semaphore()
+    for n in neighbours:
+        pl.semaphore_signal(barrier, inc=1, device_id={"lon": peer(n)}, device_id_type=MESH)
+
+    loads = []
+    for chunk in range(chunks):
+        lanes = pl.ds(chunk * width, width)
+        if not SEND_FROM_HBM:
+            load = pltpu.make_async_copy(x_hbm.at[:, :, lanes], x.at[:, :, lanes], load_sem.at[2 + chunk])
+            load.start()
+            loads.append(load)
     for chunk in range(chunks):
         lanes = pl.ds(chunk * width, width)
         pltpu.make_async_copy(x_hbm.at[:, me, lanes], g.at[:, me, lanes], recv_sem.at[0, chunk]).start()
-    load_first = pltpu.make_async_copy(first_hbm, first, load_sem.at[1])
+    load_first = pltpu.make_async_copy(first_hbm, first, load_sem.at[0])
     load_first.start()
-    load_second = pltpu.make_async_copy(second_hbm, second, load_sem.at[2])
+    load_second = pltpu.make_async_copy(second_hbm, second, load_sem.at[1])
     load_second.start()
 
-    barrier = pltpu.get_barrier_semaphore()
-
-    def greet(i, carry):
-        pl.semaphore_signal(barrier, inc=1, device_id={"lon": peer(i)}, device_id_type=MESH)
-        return carry
-
-    lax.fori_loop(0, others, greet, 0)
-    pl.semaphore_wait(barrier, others)
-    load.wait()
-
-    for chunk in range(chunks):
-        lanes = pl.ds(chunk * width, width)
-
-        def send_in(i, carry):
-            to = peer(i)
-            pltpu.make_async_remote_copy(
-                src_ref=x.at[:, to, lanes],
-                dst_ref=g.at[:, me, lanes],
-                send_sem=send_sem.at[0],
-                recv_sem=recv_sem.at[0, chunk],
-                device_id={"lon": to},
-                device_id_type=MESH,
-            ).start()
-            return carry
-
-        lax.fori_loop(0, others, send_in, 0)
+    def send_in(chunk, offset):
+        to = peer(offset)
+        lanes = pl.ds(chunk * width, width)
+        pltpu.make_async_remote_copy(
+            src_ref=(x_hbm if SEND_FROM_HBM else x).at[:, to, lanes],
+            dst_ref=g.at[:, me, lanes],
+            send_sem=send_sem.at[0],
+            recv_sem=recv_sem.at[0, chunk],
+            device_id={"lon": to},
+            device_id_type=MESH,
+        ).start()
+
+    pl.semaphore_wait(barrier, len(neighbours))
+    farthest = xs // 2 + zs // 2
+    for radius in range(1, farthest + 1):
+        if radius < farthest:
+            for n in neighbours:
+                pl.semaphore_signal(ready_sem.at[radius - 1], inc=1, device_id={"lon": peer(n)}, device_id_type=MESH)
+        if radius == 1 and loads:
+            loads[0].wait()
+        for offset in arrange(shape, IN_ORDERS[0]):
+            if steps_away(offset, shape) == radius:
+                send_in(0, offset)
+        if radius == BOTH and loads:
+            loads[1].wait()
+        if radius <= BOTH:
+            for offset in arrange(shape, IN_ORDERS[0]):
+                if steps_away(offset, shape) == radius:
+                    send_in(1, offset)
+        if radius < farthest:
+            pl.semaphore_wait(ready_sem.at[radius - 1], len(neighbours))
+    for chunk in range(1, chunks):
+        if loads and not BOTH:
+            loads[chunk].wait()
+        for offset in arrange(shape, IN_ORDERS[1]):
+            if steps_away(offset, shape) > BOTH:
+                send_in(chunk, offset)
 
     load_first.wait()
     load_second.wait()
@@ -152,28 +206,25 @@
 
         blocks = devices // kept
 
-        def send_out(i, carry):
-            to = peer(i)
+        for offset in arrange(shape, OUT_ORDERS[chunk]):
+            to = peer(offset)
             pltpu.make_async_remote_copy(
                 src_ref=o.at[:, pl.ds(to % blocks * kept, kept), to // blocks, lanes],
-                dst_ref=out_hbm.at[:, :, me, lanes],
+                dst_ref=out.at[:, :, me, lanes],
                 send_sem=send_sem.at[1],
                 recv_sem=recv_sem.at[1, chunk],
                 device_id={"lon": to},
                 device_id_type=MESH,
             ).start()
-            return carry
-
-        lax.fori_loop(0, others, send_out, 0)
         pltpu.make_async_copy(
             o.at[:, pl.ds(me % blocks * kept, kept), me // blocks, lanes],
-            out_hbm.at[:, :, me, lanes],
+            out.at[:, :, me, lanes],
             recv_sem.at[1, chunk],
         ).start()
 
     for chunk in range(chunks):
         lanes = pl.ds(chunk * width, width)
-        landed = out_hbm.at[:, :, :, lanes]
+        landed = out.at[:, :, :, lanes]
         pltpu.make_async_copy(landed, landed, recv_sem.at[1, chunk]).wait()
     sent = o.at[:, pl.ds(0, others)]
     pltpu.make_async_copy(sent, sent, send_sem.at[0]).wait()
@@ -193,7 +244,7 @@
             functools.partial(kernel, sizes),
             out_shape=jax.ShapeDtypeStruct((2, kept, fields, lats), jnp.float32),
             in_specs=[pl.BlockSpec(memory_space=pl.ANY)] * 3,
-            out_specs=pl.BlockSpec(memory_space=pl.ANY),
+            out_specs=pl.BlockSpec(memory_space=pltpu.VMEM),
             scratch_shapes=[
                 pltpu.VMEM((depth, fields, lats), jnp.float32),
                 pltpu.VMEM((depth, devices, lats), jnp.float32),
@@ -201,15 +252,16 @@
                 pltpu.VMEM((2, devices, kept, lats), jnp.float32),
                 pltpu.VMEM(first.shape, jnp.bfloat16),
                 pltpu.VMEM(second.shape, jnp.bfloat16),
-                pltpu.SemaphoreType.DMA((3,)),
+                pltpu.SemaphoreType.DMA((2 + chunks,)),
                 pltpu.SemaphoreType.DMA((2,)),
                 pltpu.SemaphoreType.DMA((2, chunks)),
+                pltpu.SemaphoreType.REGULAR((devices // 8 + 4,)),
             ],
             compiler_params=pltpu.CompilerParams(
-                collective_id=0, has_side_effects=True, vmem_limit_bytes=56 * 1024 * 1024
+                collective_id=0, has_side_effects=True, vmem_limit_bytes=16 * 1024 * 1024
             ),
             name="spectrum",
-        )(state, jnp.asarray(first), jnp.asarray(second))
+        )(*(pltpu.with_memory_space_constraint(array, pltpu.HBM) for array in (state, jnp.asarray(first), jnp.asarray(second))))
 
     return jax.shard_map(
         local,

time: 105 us -> 101 us (0.962)
  Pallas kernels: 102 us -> 99.9 us
  local copies, waits for them, and re-layouts: 3.13 us -> 1.32 us
    pallas_call x1, Pallas kernels: 102 us -> 99.9 us  [local(): pl.pallas_call(functools.partial(kernel, sizes), out_shape=jax.ShapeDtype...]
    unnamed x1, local copies, waits for them, and re-layouts: 3.13 us -> 1.32 us
where the time goes in v2:
time: 101 us
  Pallas kernels  99.9 us (99%)
  local copies, waits for them, and re-layouts  1.32 us (1%)
    pallas_call x1, Pallas kernels, local(): pl.pallas_call(functools.partial(kernel, sizes), out_shape=jax.ShapeDtype...  99.9 us

profile of v2, /device:TPU:1, one launch (start us, length us, event | category | flops | bytes accessed | tf_op | source)
XLA Modules:
  0.0 101.2 jit_solution(16528151725756361349)
XLA Ops:
  0.0 99.9 %spectrum.1 = f32[2,16,64,256]{3,2,1,0:T(8,128)S(1)} custom-call(f32[32,64,256]{2,1,0:T(8,128)} %x_hbm.1, bf16[64,192]{1,0:T(8,128)(2,1)} %constant.4.clone.first_hbm, bf16[32,64,192]{2,1,0:T(8,128)(2,1)} %constant.5.clone.second_hbm), custom_call_target="tpu_custom_call" | custom-call | tf_op jit(solution)/shard_map/spectrum/pallas_call | solution.py:243
  99.9 1.3 %copy.5 = f32[2,16,64,256]{3,2,1,0:T(8,128)} copy(f32[2,16,64,256]{3,2,1,0:T(8,128)S(1)} %spectrum.1) | data formatting | bytes 4194304

commit v3 on v2

--- a/solution.py
+++ b/solution.py
@@ -56,8 +56,10 @@
 
 SEND_FROM_HBM = False
 BOTH = 1
-IN_ORDERS = ("near", "near")
-OUT_ORDERS = ("mixback", "mixback")
+WINDOW = 2
+RANK = (0, 1, 2, 2, 3, 3, 3, 3)
+IN_ORDERS = ("near", "end_far")
+OUT_ORDERS = ("end_far", "end_far")
 
 
 def ring(step, size):
@@ -81,12 +83,34 @@
         return sorted(offsets, key=lambda o: ring(o[1], zs), reverse=True)
     if order == "znear":
         return sorted(offsets, key=lambda o: ring(o[1], zs))
+    if order == "end_far":
+        return sorted(offsets[::-1], key=lambda o: -ring(o[0], xs))
     return offsets[::-1] if order == "mixback" else offsets
 
 
 def steps_away(offset, shape):
     hops = ring(offset[0], shape[0]) + ring(offset[1], shape[1])
     return max(hops, 1)
+
+
+def ranked(shape, order, at_z):
+    zs = shape[1]
+    passes = list(dict.fromkeys((o[0], o[2]) for o in order))
+    head = [o for o in order if (o[0], o[2]) not in passes[-WINDOW:]]
+    tail = [o for o in order if (o[0], o[2]) in passes[-WINDOW:]]
+    ways = [[], [], []]
+    for o in tail:
+        if o[1] == 0:
+            ways[0].append(o)
+        elif o[1] * 2 == zs:
+            ways[1 + (o[0] + o[2] + at_z) % 2].append(o)
+        else:
+            ways[1 if o[1] * 2 < zs else 2].append(o)
+    for way in ways[1:]:
+        way.sort(key=lambda o: (RANK[(at_z + o[1]) % zs], -ring(o[1], zs)))
+    turns = [o for pair in zip(ways[1], ways[2]) for o in pair]
+    longer = max(ways[1:], key=len)
+    return head + ways[0] + turns + longer[len(turns) // 2 :]
 
 
 def kernel(sizes, x_hbm, first_hbm, second_hbm, out, x, g, middle, o, first, second, load_sem, send_sem, recv_sem, ready_sem):
@@ -206,7 +230,7 @@
 
         blocks = devices // kept
 
-        for offset in arrange(shape, OUT_ORDERS[chunk]):
+        def send_out(offset):
             to = peer(offset)
             pltpu.make_async_remote_copy(
                 src_ref=o.at[:, pl.ds(to % blocks * kept, kept), to // blocks, lanes],
@@ -216,6 +240,19 @@
                 device_id={"lon": to},
                 device_id_type=MESH,
             ).start()
+
+        order = arrange(shape, OUT_ORDERS[chunk])
+        if chunk < chunks - 1:
+            for offset in order:
+                send_out(offset)
+        else:
+            for at_z in range(zs):
+
+                @pl.when(my_z == at_z)
+                def _():
+                    for offset in ranked(shape, order, at_z):
+                        send_out(offset)
+
         pltpu.make_async_copy(
             o.at[:, pl.ds(me % blocks * kept, kept), me // blocks, lanes],
             out.at[:, :, me, lanes],

time: 101 us -> 100 us (0.990)
  Pallas kernels: 99.9 us -> 98.6 us
    pallas_call x1, Pallas kernels: 99.9 us -> 98.6 us  [local(): pl.pallas_call(functools.partial(kernel, sizes), out_shape=jax.ShapeDtype...]
where the time goes in v3:
time: 100 us; the launch traced here: 99.9 us
  Pallas kernels  98.6 us (99%)
  local copies, waits for them, and re-layouts  1.32 us (1%)
    pallas_call x1, Pallas kernels, local(): pl.pallas_call(functools.partial(kernel, sizes), out_shape=jax.ShapeDtype...  98.6 us

profile of v3, /device:TPU:1, one launch (start us, length us, event | category | flops | bytes accessed | tf_op | source)
XLA Modules:
  0.0 99.9 jit_solution(5754481199373685418)
XLA Ops:
  0.0 98.6 %spectrum.1 = f32[2,16,64,256]{3,2,1,0:T(8,128)S(1)} custom-call(f32[32,64,256]{2,1,0:T(8,128)} %x_hbm.1, bf16[64,192]{1,0:T(8,128)(2,1)} %constant.4.clone.first_hbm, bf16[32,64,192]{2,1,0:T(8,128)(2,1)} %constant.5.clone.second_hbm), custom_call_target="tpu_custom_call" | custom-call | tf_op jit(solution)/shard_map/spectrum/pallas_call | solution.py:280
  98.6 1.3 %copy.5 = f32[2,16,64,256]{3,2,1,0:T(8,128)} copy(f32[2,16,64,256]{3,2,1,0:T(8,128)S(1)} %spectrum.1) | data formatting | bytes 4194304

commit v4 on v2

--- a/solution.py
+++ b/solution.py
@@ -54,39 +54,54 @@
     return jnp.concatenate([high, high, low], axis=0)
 
 
-SEND_FROM_HBM = False
-BOTH = 1
-IN_ORDERS = ("near", "near")
-OUT_ORDERS = ("mixback", "mixback")
+RANK = (0, 1, 2, 2, 3, 3, 3, 3)
+LAST_PASSES = 2
 
 
 def ring(step, size):
     return min(step % size, -step % size)
 
 
-def arrange(shape, order):
+def hops(offset, shape):
+    return max(ring(offset[0], shape[0]) + ring(offset[1], shape[1]), 1)
+
+
+def offsets_of(shape):
     xs, zs, cores = shape
-    offsets = [
+    return [
         (dx, dz, dc)
         for dc in range(cores)
         for dx in sorted(range(xs), key=lambda d: (ring(d, xs), d))
         for dz in sorted(range(zs), key=lambda d: (ring(d, zs), d))
     ][1:]
-    distance = lambda o: ring(o[0], xs) + ring(o[1], zs) + o[2]
-    if order == "near":
-        return sorted(offsets, key=distance)
-    if order == "far":
-        return sorted(offsets, key=distance, reverse=True)
-    if order == "zfar":
-        return sorted(offsets, key=lambda o: ring(o[1], zs), reverse=True)
-    if order == "znear":
-        return sorted(offsets, key=lambda o: ring(o[1], zs))
-    return offsets[::-1] if order == "mixback" else offsets
-
-
-def steps_away(offset, shape):
-    hops = ring(offset[0], shape[0]) + ring(offset[1], shape[1])
-    return max(hops, 1)
+
+
+def near_first(shape):
+    return sorted(offsets_of(shape), key=lambda o: ring(o[0], shape[0]) + ring(o[1], shape[1]) + o[2])
+
+
+def far_first(shape):
+    return sorted(offsets_of(shape)[::-1], key=lambda o: -ring(o[0], shape[0]))
+
+
+def ranked(shape, at_z):
+    zs = shape[1]
+    order = far_first(shape)
+    passes = list(dict.fromkeys((o[0], o[2]) for o in order))
+    head = [o for o in order if (o[0], o[2]) not in passes[-LAST_PASSES:]]
+    here, up, down = [], [], []
+    for o in order[len(head) :]:
+        if o[1] == 0:
+            here.append(o)
+        elif o[1] * 2 == zs:
+            (down if (o[0] + o[2] + at_z) % 2 else up).append(o)
+        else:
+            (up if o[1] * 2 < zs else down).append(o)
+    for way in (up, down):
+        way.sort(key=lambda o: (RANK[(at_z + o[1]) % zs], -ring(o[1], zs)))
+    turns = [o for pair in zip(up, down) for o in pair]
+    longer = max((up, down), key=len)
+    return head + here + turns + longer[len(turns) // 2 :]
 
 
 def kernel(sizes, x_hbm, first_hbm, second_hbm, out, x, g, middle, o, first, second, load_sem, send_sem, recv_sem, ready_sem):
@@ -109,7 +124,7 @@
         dx, dz, dc = offset
         return part_x[dx] + part_z[dz] + part_core[dc]
 
-    neighbours = [n for n in arrange(shape, "near") if steps_away(n, shape) == 1]
+    neighbours = [n for n in near_first(shape) if hops(n, shape) == 1]
 
     barrier = pltpu.get_barrier_semaphore()
     for n in neighbours:
@@ -118,10 +133,9 @@
     loads = []
     for chunk in range(chunks):
         lanes = pl.ds(chunk * width, width)
-        if not SEND_FROM_HBM:
-            load = pltpu.make_async_copy(x_hbm.at[:, :, lanes], x.at[:, :, lanes], load_sem.at[2 + chunk])
-            load.start()
-            loads.append(load)
+        load = pltpu.make_async_copy(x_hbm.at[:, :, lanes], x.at[:, :, lanes], load_sem.at[2 + chunk])
+        load.start()
+        loads.append(load)
     for chunk in range(chunks):
         lanes = pl.ds(chunk * width, width)
         pltpu.make_async_copy(x_hbm.at[:, me, lanes], g.at[:, me, lanes], recv_sem.at[0, chunk]).start()
@@ -134,7 +148,7 @@
         to = peer(offset)
         lanes = pl.ds(chunk * width, width)
         pltpu.make_async_remote_copy(
-            src_ref=(x_hbm if SEND_FROM_HBM else x).at[:, to, lanes],
+            src_ref=x.at[:, to, lanes],
             dst_ref=g.at[:, me, lanes],
             send_sem=send_sem.at[0],
             recv_sem=recv_sem.at[0, chunk],
@@ -148,24 +162,17 @@
         if radius < farthest:
             for n in neighbours:
                 pl.semaphore_signal(ready_sem.at[radius - 1], inc=1, device_id={"lon": peer(n)}, device_id_type=MESH)
-        if radius == 1 and loads:
-            loads[0].wait()
-        for offset in arrange(shape, IN_ORDERS[0]):
-            if steps_away(offset, shape) == radius:
-                send_in(0, offset)
-        if radius == BOTH and loads:
-            loads[1].wait()
-        if radius <= BOTH:
-            for offset in arrange(shape, IN_ORDERS[0]):
-                if steps_away(offset, shape) == radius:
-                    send_in(1, offset)
+        for chunk in range(chunks if radius == 1 else 1):
+            if radius == 1:
+                loads[chunk].wait()
+            for offset in near_first(shape):
+                if hops(offset, shape) == radius:
+                    send_in(chunk, offset)
         if radius < farthest:
             pl.semaphore_wait(ready_sem.at[radius - 1], len(neighbours))
     for chunk in range(1, chunks):
-        if loads and not BOTH:
-            loads[chunk].wait()
-        for offset in arrange(shape, IN_ORDERS[1]):
-            if steps_away(offset, shape) > BOTH:
+        for offset in far_first(shape):
+            if hops(offset, shape) > 1:
                 send_in(chunk, offset)
 
     load_first.wait()
@@ -206,7 +213,7 @@
 
         blocks = devices // kept
 
-        for offset in arrange(shape, OUT_ORDERS[chunk]):
+        def send_out(offset):
             to = peer(offset)
             pltpu.make_async_remote_copy(
                 src_ref=o.at[:, pl.ds(to % blocks * kept, kept), to // blocks, lanes],
@@ -216,6 +223,18 @@
                 device_id={"lon": to},
                 device_id_type=MESH,
             ).start()
+
+        if chunk < chunks - 1:
+            for offset in far_first(shape):
+                send_out(offset)
+        else:
+            for at_z in range(zs):
+
+                @pl.when(my_z == at_z)
+                def _():
+                    for offset in ranked(shape, at_z):
+                        send_out(offset)
+
         pltpu.make_async_copy(
             o.at[:, pl.ds(me % blocks * kept, kept), me // blocks, lanes],
             out.at[:, :, me, lanes],
@@ -255,7 +274,7 @@
                 pltpu.SemaphoreType.DMA((2 + chunks,)),
                 pltpu.SemaphoreType.DMA((2,)),
                 pltpu.SemaphoreType.DMA((2, chunks)),
-                pltpu.SemaphoreType.REGULAR((devices // 8 + 4,)),
+                pltpu.SemaphoreType.REGULAR((sizes[0] // 2 + sizes[1] // 2 - 1,)),
             ],
             compiler_params=pltpu.CompilerParams(
                 collective_id=0, has_side_effects=True, vmem_limit_bytes=16 * 1024 * 1024

time: 101 us -> 100 us (0.990)
  Pallas kernels: 99.9 us -> 98.5 us
    pallas_call x1, Pallas kernels: 99.9 us -> 98.5 us  [local(): pl.pallas_call(functools.partial(kernel, sizes), out_shape=jax.ShapeDtype...]
where the time goes in v4:
time: 100 us; the launch traced here: 99.8 us
  Pallas kernels  98.5 us (98%)
  local copies, waits for them, and re-layouts  1.32 us (1%)
    pallas_call x1, Pallas kernels, local(): pl.pallas_call(functools.partial(kernel, sizes), out_shape=jax.ShapeDtype...  98.5 us

profile of v4, /device:TPU:1, one launch (start us, length us, event | category | flops | bytes accessed | tf_op | source)
XLA Modules:
  0.0 99.8 jit_solution(17549933000464455552)
XLA Ops:
  0.0 98.5 %spectrum.1 = f32[2,16,64,256]{3,2,1,0:T(8,128)S(1)} custom-call(f32[32,64,256]{2,1,0:T(8,128)} %x_hbm.1, bf16[64,192]{1,0:T(8,128)(2,1)} %constant.4.clone.first_hbm, bf16[32,64,192]{2,1,0:T(8,128)(2,1)} %constant.5.clone.second_hbm), custom_call_target="tpu_custom_call" | custom-call | tf_op jit(solution)/shard_map/spectrum/pallas_call | solution.py:262
  98.5 1.3 %copy.5 = f32[2,16,64,256]{3,2,1,0:T(8,128)} copy(f32[2,16,64,256]{3,2,1,0:T(8,128)S(1)} %spectrum.1) | data formatting | bytes 4194304

commit v5 on v4

--- a/solution.py
+++ b/solution.py
@@ -63,7 +63,8 @@
 
 
 def hops(offset, shape):
-    return max(ring(offset[0], shape[0]) + ring(offset[1], shape[1]), 1)
+    flip = offset[2] if offset[1] == 0 else 0
+    return ring(offset[0], shape[0]) + ring(offset[1], shape[1]) + flip
 
 
 def offsets_of(shape):

time: 100 us -> 100 us (level)
  no operation moved by 1% of the time
where the time goes in v5:
time: 100 us; the launch traced here: 99.4 us
  Pallas kernels  98.1 us (98%)
  local copies, waits for them, and re-layouts  1.32 us (1%)
    pallas_call x1, Pallas kernels, local(): pl.pallas_call(functools.partial(kernel, sizes), out_shape=jax.ShapeDtype...  98.1 us

profile of v5, /device:TPU:1, one launch (start us, length us, event | category | flops | bytes accessed | tf_op | source)
XLA Modules:
  0.0 99.4 jit_solution(9953818943987369455)
XLA Ops:
  0.0 98.1 %spectrum.1 = f32[2,16,64,256]{3,2,1,0:T(8,128)S(1)} custom-call(f32[32,64,256]{2,1,0:T(8,128)} %x_hbm.1, bf16[64,192]{1,0:T(8,128)(2,1)} %constant.4.clone.first_hbm, bf16[32,64,192]{2,1,0:T(8,128)(2,1)} %constant.5.clone.second_hbm), custom_call_target="tpu_custom_call" | custom-call | tf_op jit(solution)/shard_map/spectrum/pallas_call | solution.py:263
  98.1 1.3 %copy.5 = f32[2,16,64,256]{3,2,1,0:T(8,128)} copy(f32[2,16,64,256]{3,2,1,0:T(8,128)S(1)} %spectrum.1) | data formatting | bytes 4194304

commit v6 on v5

--- a/solution.py
+++ b/solution.py
@@ -95,11 +95,13 @@
         if o[1] == 0:
             here.append(o)
         elif o[1] * 2 == zs:
-            (down if (o[0] + o[2] + at_z) % 2 else up).append(o)
+            (up if (o[0] + o[2] + at_z) % 2 else down).append(o)
         else:
             (up if o[1] * 2 < zs else down).append(o)
     for way in (up, down):
         way.sort(key=lambda o: (RANK[(at_z + o[1]) % zs], -ring(o[1], zs)))
+    if up and down and RANK[(at_z + down[0][1]) % zs] < RANK[(at_z + up[0][1]) % zs]:
+        up, down = down, up
     turns = [o for pair in zip(up, down) for o in pair]
     longer = max((up, down), key=len)
     return head + here + turns + longer[len(turns) // 2 :]

time: 100 us -> 100 us (level)
  no operation moved by 1% of the time
where the time goes in v6:
time: 100 us; the launch traced here: 99.1 us
  Pallas kernels  97.8 us (98%)
  local copies, waits for them, and re-layouts  1.32 us (1%)
    pallas_call x1, Pallas kernels, local(): pl.pallas_call(functools.partial(kernel, sizes), out_shape=jax.ShapeDtype...  97.8 us

profile of v6, /device:TPU:1, one launch (start us, length us, event | category | flops | bytes accessed | tf_op | source)
XLA Modules:
  0.0 99.1 jit_solution(10190516103371786913)
XLA Ops:
  0.0 97.8 %spectrum.1 = f32[2,16,64,256]{3,2,1,0:T(8,128)S(1)} custom-call(f32[32,64,256]{2,1,0:T(8,128)} %x_hbm.1, bf16[64,192]{1,0:T(8,128)(2,1)} %constant.4.clone.first_hbm, bf16[32,64,192]{2,1,0:T(8,128)(2,1)} %constant.5.clone.second_hbm), custom_call_target="tpu_custom_call" | custom-call | tf_op jit(solution)/shard_map/spectrum/pallas_call | solution.py:265
  97.8 1.3 %copy.5 = f32[2,16,64,256]{3,2,1,0:T(8,128)} copy(f32[2,16,64,256]{3,2,1,0:T(8,128)S(1)} %spectrum.1) | data formatting | bytes 4194304

commit v7 on v6

--- a/solution.py
+++ b/solution.py
@@ -227,10 +227,7 @@
                 device_id_type=MESH,
             ).start()
 
-        if chunk < chunks - 1:
-            for offset in far_first(shape):
-                send_out(offset)
-        else:
+        if True:
             for at_z in range(zs):
 
                 @pl.when(my_z == at_z)

time: 100 us -> 100 us (level)
  no operation moved by 1% of the time
where the time goes in v7:
time: 100 us; the launch traced here: 99.1 us
  Pallas kernels  97.8 us (98%)
  local copies, waits for them, and re-layouts  1.32 us (1%)
    pallas_call x1, Pallas kernels, local(): pl.pallas_call(functools.partial(kernel, sizes), out_shape=jax.ShapeDtype...  97.8 us

profile of v7, /device:TPU:1, one launch (start us, length us, event | category | flops | bytes accessed | tf_op | source)
XLA Modules:
  0.0 99.1 jit_solution(7504529652948745449)
XLA Ops:
  0.0 97.8 %spectrum.1 = f32[2,16,64,256]{3,2,1,0:T(8,128)S(1)} custom-call(f32[32,64,256]{2,1,0:T(8,128)} %x_hbm.1, bf16[64,192]{1,0:T(8,128)(2,1)} %constant.4.clone.first_hbm, bf16[32,64,192]{2,1,0:T(8,128)(2,1)} %constant.5.clone.second_hbm), custom_call_target="tpu_custom_call" | custom-call | tf_op jit(solution)/shard_map/spectrum/pallas_call | solution.py:262
  97.8 1.3 %copy.5 = f32[2,16,64,256]{3,2,1,0:T(8,128)} copy(f32[2,16,64,256]{3,2,1,0:T(8,128)S(1)} %spectrum.1) | data formatting | bytes 4194304
